TPU v7x, 32 devices: a whole 2x2x4 slice. The times are simulated.
32 devices in a mesh: row: 16 (over z, y, core), col: 2 (over x).
Axes of the slice: x: 2, y: 2, z: 4, core: 2. Of those that a mesh axis runs over, the one named last changes fastest.
Arguments:
- pair: bfloat16 [256, 256, 128], P('row', 'col'), may hold values from -6 to 6
- relpos: bfloat16 [128, 128], replicated, may hold values from -4 to 4
- pair_gain: float32 [128], replicated, may hold values from 0.1 to 1.9
- bias_weight: bfloat16 [128, 12], replicated, may hold values from -0.5 to 0.5
- single: float32 [256, 384], P(('row', 'col')), may hold values from -6 to 6
- rotation_params: float32 [3, 256], P(None, ('row', 'col')), may hold values from -4 to 4
- translation: float32 [3, 256], P(None, ('row', 'col')), may hold values from -9 to 9
- residue_index: int32 [256], P(('row', 'col')), may hold values from 0 to 50944, as said below
- residue_mask: int32 [256], P(('row', 'col')), may hold values 0 or 1
- w_scalar: float32 [384, 576], replicated, may hold values from -0.3125 to 0.3125
- w_points: float32 [384, 576], replicated, may hold values from -0.3125 to 0.3125
- head_weights: float32 [12], replicated, may hold values from -2 to 1.5
- w_out: float32 [2112, 384], replicated, may hold values from -0.125 to 0.125
- w_hidden: float32 [384, 384], replicated, may hold values from -0.3125 to 0.3125
- w_back: float32 [384, 384], replicated, may hold values from -0.3125 to 0.3125
- w_frame: float32 [384, 6], replicated, may hold values from -0.078125 to 0.078125
Outputs:
- single_out: float32 [256, 384], P(('row', 'col'))
- frames: float32 [12, 256], P(None, ('row', 'col'))
Inputs may be any that keep to these rules, and one draw needn't show every extreme that they name: residue_index is strictly increasing along the crop, begins at 0 and ends at exactly 50944.
All inputs are finite; a program needn't handle non-finite values. No bound on the sum of `residue_mask` on one device may be relied on, other than what follows from the above.
Results may differ from a plain program's by a relative error of at most 0.0025.
Values may be sent and summed in bfloat16 or wider, within the bound.
A program may use at most 64 MiB of HBM per device.

v0:
```python
import math

import jax
import jax.numpy as jnp
from jax import lax
from jax.sharding import PartitionSpec as P

H = 12
C = 16
PQ = 4
PV = 8
BINS = 128
ITERS = 3


NORM_EPSILON = 1e-05
MASKED_LOGIT = -100000.0
NORM_FLOOR = 0.1
HIGHEST_PRECISION = lax.Precision.HIGHEST


def broadcast(value, axis, root):
    mine = lax.axis_index(axis) == root
    return lax.psum(jnp.where(mine, value, jnp.zeros_like(value)), axis)


def joined(part, axis, combine):
    gathered = jax.tree.map(lambda a: lax.all_gather(a, axis), part)

    def take(source):
        return jax.tree.map(lambda a: lax.dynamic_index_in_dim(a, source, 0, False), gathered)

    return lax.fori_loop(
        1, lax.axis_size(axis), lambda source, state: combine(state, take(source)), take(0)
    )


def layer_norm(values):
    center = values - jnp.mean(values, axis=-1, keepdims=True)
    spread = jnp.mean(center * center, axis=-1, keepdims=True)
    return center * lax.rsqrt(spread + NORM_EPSILON)


def rotation_from(update):
    quat_b, quat_c, quat_d = (update[0], update[1], update[2])
    inverse = 1.0 / (1.0 + quat_b * quat_b + quat_c * quat_c + quat_d * quat_d)
    entries = [
        1.0 + quat_b * quat_b - quat_c * quat_c - quat_d * quat_d,
        2.0 * (quat_b * quat_c - quat_d),
        2.0 * (quat_b * quat_d + quat_c),
        2.0 * (quat_b * quat_c + quat_d),
        1.0 - quat_b * quat_b + quat_c * quat_c - quat_d * quat_d,
        2.0 * (quat_c * quat_d - quat_b),
        2.0 * (quat_b * quat_d - quat_c),
        2.0 * (quat_c * quat_d + quat_b),
        1.0 - quat_b * quat_b - quat_c * quat_c + quat_d * quat_d,
    ]
    return jnp.stack(entries) * inverse


def to_global(rotation, points, translation):
    return jnp.stack(
        [
            rotation[3 * component] * points[0]
            + rotation[3 * component + 1] * points[1]
            + rotation[3 * component + 2] * points[2]
            + translation[component]
            for component in range(3)
        ]
    )


def to_local(rotation, points, translation):
    moved = [points[component] - translation[component] for component in range(3)]
    return jnp.stack(
        [
            rotation[component] * moved[0]
            + rotation[3 + component] * moved[1]
            + rotation[6 + component] * moved[2]
            for component in range(3)
        ]
    )


def compose(rotation, translation, update):
    turn = rotation_from(update[:3])
    new_rotation = jnp.stack(
        [
            rotation[3 * left] * turn[right]
            + rotation[3 * left + 1] * turn[3 + right]
            + rotation[3 * left + 2] * turn[6 + right]
            for left in range(3)
            for right in range(3)
        ]
    )
    new_translation = jnp.stack(
        [
            rotation[3 * left] * update[3]
            + rotation[3 * left + 1] * update[4]
            + rotation[3 * left + 2] * update[5]
            + translation[left]
            for left in range(3)
        ]
    )
    return (new_rotation, new_translation)


def project(single, rotation, translation, w_scalar, w_points):
    count = single.shape[0]
    scalars = jnp.dot(
        single, w_scalar, precision=HIGHEST_PRECISION, preferred_element_type=jnp.float32
    ).T
    scalars = scalars.reshape(3, H * C, count).astype(jnp.bfloat16)
    points = jnp.dot(
        single, w_points, precision=HIGHEST_PRECISION, preferred_element_type=jnp.float32
    ).T
    query_local = points[: 3 * H * PQ].reshape(3, H * PQ, count)
    key_local = points[3 * H * PQ : 6 * H * PQ].reshape(3, H * PQ, count)
    value_local = points[6 * H * PQ :].reshape(3, H * PV, count)
    return (
        scalars,
        to_global(rotation, query_local, translation),
        to_global(rotation, key_local, translation),
        to_global(rotation, value_local, translation),
    )


def advance(
    single, rotation, translation, scalar_out, point_out, pair_out, w_out, w_hidden, w_back, w_frame
):
    count = single.shape[0]
    local = to_local(rotation, point_out, translation)
    lengths = jnp.sqrt(jnp.sum(local * local, axis=0) + NORM_FLOOR)
    features = jnp.concatenate(
        [scalar_out, local.reshape(3 * H * PV, count), lengths, pair_out], axis=0
    )
    mixed = jnp.dot(
        features.T, w_out, precision=HIGHEST_PRECISION, preferred_element_type=jnp.float32
    )
    single = layer_norm(single + mixed)
    hidden = jax.nn.relu(
        jnp.dot(single, w_hidden, precision=HIGHEST_PRECISION, preferred_element_type=jnp.float32)
    )
    single = layer_norm(
        single
        + jnp.dot(hidden, w_back, precision=HIGHEST_PRECISION, preferred_element_type=jnp.float32)
    )
    update = jnp.dot(
        single, w_frame, precision=HIGHEST_PRECISION, preferred_element_type=jnp.float32
    ).T
    rotation, translation = compose(rotation, translation, update)
    return (single, rotation, translation)


def attend_block(
    query, keyval, query_side, key_side, value_side, bias, normed, pair_live, point_scale
):
    heads_query = query.reshape(H, C, -1)
    keys = keyval[0].reshape(H, C, -1)
    values = keyval[1].reshape(H, C, -1)
    query_grid = query_side.reshape(3, H, PQ, -1)
    key_grid = key_side.reshape(3, H, PQ, -1)
    value_grid = value_side.reshape(3, H, PV, -1)
    scores = jnp.einsum(
        "hci,hcj->hij", heads_query, keys, preferred_element_type=jnp.float32
    ) / math.sqrt(C)
    cross = jnp.einsum("ahpi,ahpj->hij", query_grid, key_grid, precision=HIGHEST_PRECISION)
    distance = (
        jnp.sum(query_grid * query_grid, axis=(0, 2))[:, :, None]
        + jnp.sum(key_grid * key_grid, axis=(0, 2))[:, None, :]
        - 2.0 * cross
    )
    logits = math.sqrt(1.0 / 3.0) * (scores + bias - point_scale[:, None, None] * distance)
    logits = jnp.where(pair_live[None], logits, MASKED_LOGIT)
    local_max = jnp.max(logits, axis=-1)
    unscaled = jnp.exp(logits - local_max[:, :, None])
    total_weight = jnp.sum(unscaled, axis=-1)
    rounded = unscaled.astype(jnp.bfloat16)
    scalar_sum = jnp.einsum("hij,hcj->hci", rounded, values, preferred_element_type=jnp.float32)
    point_sum = jnp.einsum("hij,ahpj->ahpi", unscaled, value_grid, precision=HIGHEST_PRECISION)
    pair_sum = jnp.einsum("hij,ijc->hci", rounded, normed, preferred_element_type=jnp.float32)
    return (local_max, total_weight, scalar_sum, point_sum, pair_sum)


def merge_softmax(first, second):
    top = jnp.maximum(first[0], second[0])
    lead = jnp.exp(first[0] - top)
    trail = jnp.exp(second[0] - top)
    return (
        top,
        first[1] * lead + second[1] * trail,
        first[2] * lead[:, None, :] + second[2] * trail[:, None, :],
        first[3] * lead[None, :, None, :] + second[3] * trail[None, :, None, :],
        first[4] * lead[:, None, :] + second[4] * trail[:, None, :],
    )


def body(
    pair,
    relpos,
    pair_gain,
    bias_weight,
    single,
    rotation_params,
    translation,
    residue_index,
    residue_mask,
    w_scalar,
    w_points,
    head_weights,
    w_out,
    w_hidden,
    w_back,
    w_frame,
):
    row_rows = pair.shape[0]
    col_rows = pair.shape[1]
    owned = single.shape[0]
    row_place = lax.axis_index("row")
    col_place = lax.axis_index("col")
    index_all, mask_all = (
        lax.all_gather(residue_index, ("row", "col"), axis=0, tiled=True),
        lax.all_gather(residue_mask, ("row", "col"), axis=0, tiled=True),
    )
    query_index = lax.dynamic_slice_in_dim(index_all, row_place * row_rows, row_rows, 0)
    key_index = lax.dynamic_slice_in_dim(index_all, col_place * col_rows, col_rows, 0)
    query_live = lax.dynamic_slice_in_dim(mask_all, row_place * row_rows, row_rows, 0) == 1
    key_live = lax.dynamic_slice_in_dim(mask_all, col_place * col_rows, col_rows, 0) == 1
    pair_live = query_live[:, None] & key_live[None, :]
    span_rows = math.gcd(row_rows, 64)

    def prepare(index):
        offset = (
            jnp.clip(key_index[None, :] - query_index[:, None], -(BINS // 2), BINS // 2 - 1)
            + BINS // 2
        )
        onehot = (offset[:, :, None] == lax.broadcasted_iota(jnp.int32, (1, 1, BINS), 2)).astype(
            jnp.bfloat16
        )
        embedded = jnp.dot(
            onehot.reshape(span_rows * col_rows, BINS), relpos, preferred_element_type=jnp.float32
        )
        summed = pair.astype(jnp.float32) + embedded.reshape(span_rows, col_rows, -1)
        normed_part = (layer_norm(summed) * pair_gain).astype(jnp.bfloat16)
        bias_part = jnp.einsum(
            "ijc,ch->hij", normed_part, bias_weight, preferred_element_type=jnp.float32
        )
        return (normed_part, bias_part)

    normed_blocks, bias_blocks = lax.map(
        prepare, jnp.arange(row_rows // span_rows, dtype=jnp.int32)
    )
    normed = normed_blocks.reshape(row_rows, col_rows, -1)
    bias = bias_blocks.transpose(1, 0, 2, 3).reshape(H, row_rows, col_rows)
    point_scale = jax.nn.softplus(head_weights) * (math.sqrt(2.0 / (9.0 * PQ)) / 2.0)
    rotation = rotation_from(rotation_params)
    state = single
    for step in range(ITERS):
        scalars, query_points, key_points, value_points = project(
            state, rotation, translation, w_scalar, w_points
        )
        query_flat = query_points.reshape(-1, owned)
        key_flat = key_points.reshape(-1, owned)
        value_flat = value_points.reshape(-1, owned)
        block_scalar = lax.all_gather(scalars, "col", axis=2, tiled=True)
        block_point = (
            lax.all_gather(query_flat, "col", axis=1, tiled=True),
            lax.all_gather(key_flat, "col", axis=1, tiled=True),
            lax.all_gather(value_flat, "col", axis=1, tiled=True),
        )
        query = block_scalar[0]
        query_side = block_point[0]
        ratio = lax.axis_size("row") // lax.axis_size("col")
        scalar_pieces = []
        key_pieces = []
        value_pieces = []
        for part in range(ratio):
            root = col_place * ratio + part
            scalar_pieces.append(broadcast(block_scalar[1:], "row", root))
            key_piece, value_piece = (
                broadcast(block_point[1], "row", root),
                broadcast(block_point[2], "row", root),
            )
            key_pieces.append(key_piece)
            value_pieces.append(value_piece)
        keyval = jnp.concatenate(scalar_pieces, axis=2)
        key_side = jnp.concatenate(key_pieces, axis=1)
        value_side = jnp.concatenate(value_pieces, axis=1)
        local_max, total_weight, scalar_sum, point_sum, pair_sum = attend_block(
            query, keyval, query_side, key_side, value_side, bias, normed, pair_live, point_scale
        )
        pair_out = None
        merged = joined(
            (local_max, total_weight, scalar_sum, point_sum, pair_sum), "col", merge_softmax
        )
        begin = col_place * owned
        total = lax.dynamic_slice_in_dim(merged[1], begin, owned, 1)
        scalar_share = lax.dynamic_slice_in_dim(merged[2], begin, owned, 2)
        point_share = lax.dynamic_slice_in_dim(merged[3], begin, owned, 3)
        pair_share = lax.dynamic_slice_in_dim(merged[4], begin, owned, 2)
        scalar_out = (scalar_share / total[:, None, :]).reshape(H * C, owned)
        point_out = (point_share / total[None, :, None, :]).reshape(3, H * PV, owned)
        pair_out = (pair_share / total[:, None, :]).reshape(-1, owned)
        state, rotation, translation = advance(
            state,
            rotation,
            translation,
            scalar_out,
            point_out,
            pair_out,
            w_out,
            w_hidden,
            w_back,
            w_frame,
        )
    frames = jnp.concatenate([rotation, translation], axis=0)
    return (state, frames)


def solution(mesh):
    placed = (
        P("row", "col", None),
        P(),
        P(),
        P(),
        P(("row", "col"), None),
        P(None, ("row", "col")),
        P(None, ("row", "col")),
        P(("row", "col")),
        P(("row", "col")),
        P(),
        P(),
        P(),
        P(),
        P(),
        P(),
        P(),
    )
    return jax.shard_map(
        body,
        mesh=mesh,
        in_specs=placed,
        out_specs=(P(("row", "col"), None), P(None, ("row", "col"))),
        check_vma=False,
    )
```

profile of v0, /device:TPU:29, one launch (start us, length us, event | category | flops | bytes accessed | tf_op | source)
XLA Modules:
  0.0 847.5 jit_solution(17176998492599648123)
XLA Ops:
  9.6 3.2 all_gather.132
  18.8 3.2 all_gather.143
  27.2 41.6 %all-reduce.2 = (s32[256]{0:T(256)S(1)}, s32[256]{0:T(256)S(1)}) all-reduce(s32[256]{0:T(256)S(1)} %dynamic-update-slice.1, s32[256]{0:T(256)S(1)} %dynamic-update-slice), channel_id=1, replica_groups=mesh['row'=16,'col'=2] {'row','col'}, use_global_device_ids=true, to_apply=%add.1 | all-reduce | flops 512 | bytes 4096
  82.1 22.3 %all-reduce.26.cloned.1.call-done = (bf16[2,192,16]{1,2,0:T(8,128)(2,1)}, bf16[2,192,16]{1,2,0:T(8,128)(2,1)}, bf16[2,192,16]{1,2,0:T(8,128)(2,1)}, bf16[2,192,1...) async-done(((bf16[2,192,16]{1,2,0:T(8,128)(2,1)}, ...) | async-done | bytes 98320 | tf_op jit(solution)/shard_map/psum | solution.py:24
  113.1 92.5 %all-reduce.20.cloned.1.call-done = (f32[144,16]{0,1:T(8,128)}, f32[144,16]{0,1:T(8,128)}, f32[144,16]{0,1:T(8,128)}, f32[144,16]{0,1:T(8,128)}, f32[144,16]{0,1...) async-done(((f32[144,16]{0,1:T(8,128)}, f32[144,16]{0,1:T(8,128)}, ...) | async-done | bytes 221200 | tf_op jit(solution)/shard_map/psum | solution.py:24
  233.3 3.2 all-gather.15
  242.1 4.1 all-gather.4
  247.0 4.5 all-gather
  253.8 4.6 all-gather.3
  271.3 3.2 all_gather.148
  281.2 3.2 all_gather.157
  287.7 100.7 %all-reduce.24.cloned.1.call-done = (bf16[2,192,16]{1,2,0:T(8,128)(2,1)}, bf16[2,192,16]{1,2,0:T(8,128)(2,1)}, bf16[2,192,16]{1,2,0:T(8,128)(2,1)}, bf16[2,192,1...) async-done(((bf16[2,192,16]{1,2,0:T(8,128)(2,1)}, ...) | async-done | bytes 98320 | tf_op jit(solution)/shard_map/psum | solution.py:24
  397.1 92.4 %all-reduce.18.cloned.1.call-done = (f32[144,16]{0,1:T(8,128)}, f32[144,16]{0,1:T(8,128)}, f32[144,16]{0,1:T(8,128)}, f32[144,16]{0,1:T(8,128)}, f32[144,16]{0,1...) async-done(((f32[144,16]{0,1:T(8,128)}, f32[144,16]{0,1:T(8,128)}, ...) | async-done | bytes 221200 | tf_op jit(solution)/shard_map/psum | solution.py:24
  503.2 3.2 all-gather.17
  512.2 4.1 all-gather.9
  517.1 4.4 all-gather.5
  537.7 4.7 all-gather.8
  559.1 3.2 all_gather.162
  569.0 3.2 all_gather.171
  575.3 100.4 %all-reduce.22.cloned.1.call-done = (bf16[2,192,16]{1,2,0:T(8,128)(2,1)}, bf16[2,192,16]{1,2,0:T(8,128)(2,1)}, bf16[2,192,16]{1,2,0:T(8,128)(2,1)}, bf16[2,192,1...) async-done(((bf16[2,192,16]{1,2,0:T(8,128)(2,1)}, ...) | async-done | bytes 98320 | tf_op jit(solution)/shard_map/psum | solution.py:24
  684.3 92.4 %all-reduce.16.cloned.1.call-done = (f32[144,16]{0,1:T(8,128)}, f32[144,16]{0,1:T(8,128)}, f32[144,16]{0,1:T(8,128)}, f32[144,16]{0,1:T(8,128)}, f32[144,16]{0,1...) async-done(((f32[144,16]{0,1:T(8,128)}, f32[144,16]{0,1:T(8,128)}, ...) | async-done | bytes 221200 | tf_op jit(solution)/shard_map/psum | solution.py:24
  799.5 4.1 all-gather.10
  805.4 4.1 all-gather.14
  824.0 4.9 all-gather.13
  (486 shorter events, 224.1 us)
Async XLA Ops:
  7.2 255.0 %copy-start = (f32[2112,384]{1,0:T(8,128)S(1)}, f32[2112,384]{1,0:T(8,128)}, u32[]{:S(2)}) copy-start(f32[2112,384]{1,0:T(8,128)} %param.28) | copy-start | bytes 9732100
  7.2 19.6 %copy-start.66 = (s32[8]{0:T(128)S(1)}, s32[8]{0:T(128)}, u32[]{:S(2)}) copy-start(s32[8]{0:T(128)} %param.23) | copy-start | bytes 100
  7.2 19.8 %copy-start.67 = (s32[8]{0:T(128)S(1)}, s32[8]{0:T(128)}, u32[]{:S(2)}) copy-start(s32[8]{0:T(128)} %param.24) | copy-start | bytes 100
  7.2 61.9 %copy-start.68 = (f32[12]{0:T(128)S(1)}, f32[12]{0:T(128)}, u32[]{:S(2)}) copy-start(f32[12]{0:T(128)} %param.27) | copy-start | bytes 148
  7.2 69.4 %copy-start.13 = (bf16[128,128]{1,0:T(8,128)(2,1)S(1)}, bf16[128,128]{1,0:T(8,128)(2,1)}, u32[]{:S(2)}) copy-start(bf16[128,128]{1,0:T(8,128)(2,1)} %param.17) | copy-start | bytes 98308
  7.2 97.2 %all-reduce.26.cloned.1.call-start = ((), (), s32[]{:S(2)}) async-start(), calls=%async_computation.5 | async-start | bytes 262144 | tf_op jit(solution)/shard_map/psum | solution.py:24
  13.5 66.2 %copy-start.65 = (f32[128]{0:T(128)S(1)}, f32[128]{0:T(128)}, u32[]{:S(2)}) copy-start(f32[128]{0:T(128)} %param.18) | copy-start | bytes 1540
  13.5 192.0 %all-reduce.20.cloned.1.call-start = ((), (), s32[]{:S(2)}) async-start(), calls=%async_computation.2 | async-start | bytes 655360 | tf_op jit(solution)/shard_map/psum | solution.py:24
  25.3 56.6 %copy-start.64 = (bf16[128,12]{0,1:T(8,128)(2,1)S(1)}, bf16[128,12]{0,1:T(8,128)(2,1)}, u32[]{:S(2)}) copy-start(bf16[128,12]{0,1:T(8,128)(2,1)} %param.19) | copy-start | bytes 9220
  26.7 361.7 %all-reduce.24.cloned.1.call-start = ((), (), s32[]{:S(2)}) async-start(), calls=%async_computation.4 | async-start | bytes 262144 | tf_op jit(solution)/shard_map/psum | solution.py:24
  76.6 153.0 %copy-start.60 = (f32[12]{0:T(128)S(1)}, f32[12]{0:T(128)}, u32[]{:S(2)}) copy-start(f32[12]{0:T(128)} %fusion.102) | copy-start | bytes 148
  79.7 153.6 %copy-start.11 = (pred[16,128]{1,0:T(8,128)(4,1)}, pred[16,128]{1,0:T(8,128)(4,1)S(1)}, u32[]{:S(2)}) copy-start(pred[16,128]{1,0:T(8,128)(4,1)S(1)} %broadcast_and_fusion) | copy-start | bytes 6148
  286.6 202.9 %all-reduce.18.cloned.1.call-start = ((), (), s32[]{:S(2)}) async-start(), calls=%async_computation.1 | async-start | bytes 655360 | tf_op jit(solution)/shard_map/psum | solution.py:24
  287.6 388.0 %all-reduce.22.cloned.1.call-start = ((), (), s32[]{:S(2)}) async-start(), calls=%async_computation.3 | async-start | bytes 262144 | tf_op jit(solution)/shard_map/psum | solution.py:24
  503.2 40.2 %copy-start.15 = (f32[1,8]{1,0:T(1,128)S(1)}, f32[1,8]{1,0:T(1,128)}, u32[]{:S(2)}) copy-start(f32[1,8]{1,0:T(1,128)} %copy-done.14) | copy-start | bytes 100
  521.6 20.8 %copy-start.9 = (f32[12,8]{1,0:T(8,128)}, f32[12,8]{1,0:T(8,128)S(1)}, u32[]{:S(2)}) copy-start(f32[12,8]{1,0:T(8,128)S(1)} %get-tuple-element.421) | copy-start | bytes 1156
  549.3 240.1 %copy-start.12 = (pred[16,128]{1,0:T(8,128)(4,1)S(1)}, pred[16,128]{1,0:T(8,128)(4,1)}, u32[]{:S(2)}) copy-start(pred[16,128]{1,0:T(8,128)(4,1)} %copy-done.11) | copy-start | bytes 6148
  549.8 12.5 %copy-start.58 = (f32[8]{0:T(128)}, f32[8]{0:T(128)S(1)}, u32[]{:S(2)}) copy-start(f32[8]{0:T(128)S(1)} %broadcast_multiply_fusion.7) | copy-start | bytes 100
  551.6 10.7 %copy-start.42 = (f32[1,8]{1,0:T(1,128)}, f32[1,8]{1,0:T(1,128)S(1)}, u32[]{:S(2)}) copy-start(f32[1,8]{1,0:T(1,128)S(1)} %get-tuple-element.447) | copy-start | bytes 100
  552.3 10.0 %copy-start.43 = (f32[1,8]{1,0:T(1,128)}, f32[1,8]{1,0:T(1,128)S(1)}, u32[]{:S(2)}) copy-start(f32[1,8]{1,0:T(1,128)S(1)} %get-tuple-element.452) | copy-start | bytes 100
  574.4 202.3 %all-reduce.16.cloned.1.call-start = ((), (), s32[]{:S(2)}) async-start(), calls=%async_computation | async-start | bytes 655360 | tf_op jit(solution)/shard_map/psum | solution.py:24
  790.4 39.4 %copy-start.19 = (f32[1,8]{1,0:T(1,128)S(1)}, f32[1,8]{1,0:T(1,128)}, u32[]{:S(2)}) copy-start(f32[1,8]{1,0:T(1,128)} %copy-done.18) | copy-start | bytes 100
  790.4 39.4 %copy-start.21 = (f32[1,8]{1,0:T(1,128)S(1)}, f32[1,8]{1,0:T(1,128)}, u32[]{:S(2)}) copy-start(f32[1,8]{1,0:T(1,128)} %copy-done.20) | copy-start | bytes 100
  790.4 39.4 %copy-start.23 = (f32[1,8]{1,0:T(1,128)S(1)}, f32[1,8]{1,0:T(1,128)}, u32[]{:S(2)}) copy-start(f32[1,8]{1,0:T(1,128)} %copy-done.22) | copy-start | bytes 100
  (51 other events, 268.5 us)
Sparse Core Ops, SparseCore 0:
  13.6 90.7 all-reduce.25
  109.6 95.8 all-reduce.19
  286.7 101.6 all-reduce.23
  393.5 95.9 all-reduce.17
  574.5 101.0 all-reduce.21
  680.7 95.9 all-reduce.15
where the time goes:
time: 862 us; the launch traced here: 847 us
  waiting for transfers between devices  501 us (58%)
  blocking collectives  139 us (16%)
  local copies, waits for them, and re-layouts  119 us (14%)
  matrix products  43.3 us (5%)
  other arithmetic  29.7 us (3%)
  between operations  15.7 us (2%)
    psum x6, waiting for transfers between devices, broadcast(): return lax.psum(jnp.where(mine, value, jnp.zeros_like(value)), axis)  501 us
    unnamed x207, local copies, waits for them, and re-layouts  76.3 us
    all_gather x15, blocking collectives, joined(): gathered = jax.tree.map(lambda a: lax.all_gather(a, axis), part)  58.9 us
    unnamed x1, blocking collectives  41.6 us
  transfers between devices with their start and end apart: 6, of which 6 were waited for; matrix products, arithmetic and copies ran while one was open for 5% of the time, Pallas kernels for 0%

commit v1 on v0

v1 whole, which is shorter than its diff:
```python
import functools
import math

import jax
import jax.numpy as jnp
from jax import lax
from jax.experimental import pallas as pl
from jax.experimental.pallas import tpu as pltpu
from jax.sharding import PartitionSpec as P

H = 12
HP = 16
C = 16
PQ = 4
PV = 8
BINS = 128
ITERS = 3
D = 384
WIDE = 512
NORM_EPSILON = 1e-05
MASKED_LOGIT = -100000.0
NORM_FLOOR = 0.1
MESH = pl.DeviceIdType.MESH
F32 = jnp.float32
BF16 = jnp.bfloat16
NN = (((1,), (0,)), ((), ()))
NT = (((1,), (1,)), ((), ()))
INDEX_AT = 12
MASK_AT = 13


def rotation_from(quat_b, quat_c, quat_d):
    inverse = 1.0 / (1.0 + quat_b * quat_b + quat_c * quat_c + quat_d * quat_d)
    entries = [
        1.0 + quat_b * quat_b - quat_c * quat_c - quat_d * quat_d,
        2.0 * (quat_b * quat_c - quat_d),
        2.0 * (quat_b * quat_d + quat_c),
        2.0 * (quat_b * quat_c + quat_d),
        1.0 - quat_b * quat_b + quat_c * quat_c - quat_d * quat_d,
        2.0 * (quat_c * quat_d - quat_b),
        2.0 * (quat_b * quat_d - quat_c),
        2.0 * (quat_c * quat_d + quat_b),
        1.0 - quat_b * quat_b - quat_c * quat_c + quat_d * quat_d,
    ]
    return [entry * inverse for entry in entries]


def layer_norm(values):
    center = values - jnp.mean(values, axis=-1, keepdims=True)
    spread = jnp.mean(center * center, axis=-1, keepdims=True)
    return center * lax.rsqrt(spread + NORM_EPSILON)


def split(x):
    high = x.astype(BF16)
    return high, (x - high.astype(F32)).astype(BF16)


def mm(a, b, dims=NN):
    return lax.dot_general(a, b, dims, preferred_element_type=F32)


def mm3(a, b, dims=NN):
    return mm(a[0], b[0], dims) + (mm(a[0], b[1], dims) + mm(a[1], b[0], dims))


def head_mask(width):
    head = lax.broadcasted_iota(jnp.int32, (HP, H * width), 0) * width
    lane = lax.broadcasted_iota(jnp.int32, (HP, H * width), 1)
    return ((lane >= head) & (lane < head + width)).astype(F32)


def spread_heads(rows, mask):
    return jnp.concatenate(
        [rows[i : i + 1] * mask for i in range(rows.shape[0])], axis=0
    )


def pick_heads(rows, mask):
    width = rows.shape[1]
    return jnp.sum(rows.reshape(-1, HP, width) * mask[None], axis=1)


def kernel(
    nrow,
    ncol,
    s0_ref,
    pair_ref,
    relpos_ref,
    gain_ref,
    bw_ref,
    ps_ref,
    ws_ref,
    wp_ref,
    wo_ref,
    wh_ref,
    wb_ref,
    wf_ref,
    single_ref,
    frames_ref,
    state,
    gathered,
    pairs,
    normed,
    bias,
    pair_out,
    wst,
    wpt,
    wo2,
    wh2,
    wb2,
    pair_send,
    pair_recv,
    pair_local,
    state_send,
    state_recv,
):
    n = nrow * ncol
    row = lax.axis_index("row")
    col = lax.axis_index("col")
    me = row * ncol + col
    owned = s0_ref.shape[0]
    count = n * owned
    col_rows = pair_ref.shape[1]

    barrier = pltpu.get_barrier_semaphore()

    def greet(k, carry):
        other = lax.rem(me + k, n)
        pl.semaphore_signal(
            barrier, inc=1, device_id=(other // ncol, lax.rem(other, ncol)), device_id_type=MESH
        )
        return carry

    lax.fori_loop(1, n, greet, 0)

    my_rows = pl.ds(pl.multiple_of(me * owned, owned), owned)
    my_cols = pl.ds(pl.multiple_of(col * col_rows, col_rows), col_rows)

    def state_copy(step, k):
        other = lax.rem(me + k, n)
        return pltpu.make_async_remote_copy(
            src_ref=state.at[step],
            dst_ref=gathered.at[step, my_rows],
            send_sem=state_send.at[step],
            recv_sem=state_recv.at[step],
            device_id=(other // ncol, lax.rem(other, ncol)),
            device_id_type=MESH,
        )

    def send_state(step):
        def one(k, carry):
            state_copy(step, k).start()
            return carry

        lax.fori_loop(1, n, one, 0)

    def wait_all(step, sem):
        part = gathered.at[step, pl.ds(0, (n - 1) * owned)]
        pltpu.make_async_copy(part, part, sem.at[step]).wait()

    state[0] = s0_ref[...]
    gathered[0, my_rows] = s0_ref[...]
    own_pair = pltpu.make_async_copy(
        pair_ref.at[pl.ds(col * owned, owned)], pairs.at[:, my_cols], pair_local
    )
    own_pair.start()
    pl.semaphore_wait(barrier, n - 1)
    send_state(0)
    for k in range(1, ncol):
        other = lax.rem(col + k, ncol)
        pltpu.make_async_remote_copy(
            src_ref=pair_ref.at[pl.ds(other * owned, owned)],
            dst_ref=pairs.at[:, my_cols],
            send_sem=pair_send,
            recv_sem=pair_recv,
            device_id=(row, other),
            device_id_type=MESH,
        ).start()

    for source, target in ((ws_ref, wst), (wp_ref, wpt)):
        total = source.shape[1]
        for begin in range(0, total, 128):
            end = min(begin + 128, total)
            high, low = split(source[:, begin:end].T)
            target[0, begin:end] = high
            target[1, begin:end] = low
    for source, target in ((wo_ref, wo2), (wh_ref, wh2), (wb_ref, wb2)):
        high, low = split(source[...])
        target[0] = high
        target[1] = low

    own_pair.wait()
    if ncol > 1:
        part = pairs.at[:, pl.ds(0, (ncol - 1) * col_rows)]
        pltpu.make_async_copy(part, part, pair_recv).wait()
    wait_all(0, state_recv)

    index_col = gathered[0, :, D : D + 128][:, INDEX_AT : INDEX_AT + 1]
    lanes = lax.broadcasted_iota(jnp.int32, (count, BINS), 1).astype(F32)
    own_index = s0_ref[:, D:][:, INDEX_AT : INDEX_AT + 1]
    sublanes = lax.broadcasted_iota(jnp.int32, (owned, 1), 0)
    relpos = relpos_ref[...]
    gain = gain_ref[...]
    bw = bw_ref[...]

    def prepare(i, carry):
        mine = jnp.sum(jnp.where(sublanes == i, own_index, 0.0), axis=0, keepdims=True)
        offset = jnp.clip(index_col - mine, -(BINS // 2), BINS // 2 - 1) + BINS // 2
        onehot = (offset == lanes).astype(F32).astype(BF16)
        summed = pairs[i].astype(F32) + mm(onehot, relpos)
        rows = (layer_norm(summed) * gain).astype(BF16)
        normed[i] = rows
        bias[i] = mm(bw, rows, NT)
        return carry

    lax.fori_loop(0, owned, prepare, 0)

    def dense(x, weight, begin, size):
        high, low = split(x)
        stacked = jnp.concatenate([high.astype(F32), low.astype(F32)], axis=0).astype(BF16)
        both = mm(stacked, weight[0, begin : begin + size])
        return both[:owned] + both[owned:] + mm(high, weight[1, begin : begin + size])

    def step_body(step, carry):
        @pl.when(step > 0)
        def _():
            wait_all(step, state_recv)

        turned = gathered[step].T
        x = split(turned[:D])
        frame = [turned[D + k : D + k + 1] for k in range(14)]
        mine = state[step]
        own = mine[:, :D]
        block = mine[:, D:]
        rot = [block[:, k : k + 1] for k in range(9)]
        pos = [block[:, 9 + k : 10 + k] for k in range(3)]
        own2 = split(own)
        hc = H * C
        keyval = mm3((wst[0, hc:], wst[1, hc:]), x).astype(BF16)
        keys, values = keyval[:hc], keyval[hc:]
        kp = 3 * H * PQ
        locals_t = mm3((wpt[0, kp:], wpt[1, kp:]), x)

        def lift(base, width):
            p = [locals_t[base + a * width : base + (a + 1) * width] for a in range(3)]
            return [
                frame[3 * a] * p[0] + frame[3 * a + 1] * p[1] + frame[3 * a + 2] * p[2] + frame[9 + a]
                for a in range(3)
            ]

        key_points = lift(0, H * PQ)
        value_points = lift(kp, H * PV)
        query = mm3(own2, (wst[0, :hc], wst[1, :hc]), NT).astype(BF16).astype(F32)
        q = [
            mm3(
                own2,
                (
                    wpt[0, a * H * PQ : (a + 1) * H * PQ],
                    wpt[1, a * H * PQ : (a + 1) * H * PQ],
                ),
                NT,
            )
            for a in range(3)
        ]
        query_points = [
            rot[3 * a] * q[0] + rot[3 * a + 1] * q[1] + rot[3 * a + 2] * q[2] + pos[a]
            for a in range(3)
        ]
        mask_c, mask_q, mask_v = head_mask(C), head_mask(PQ), head_mask(PV)
        scores = mm(spread_heads(query, mask_c).astype(BF16), keys) * (1.0 / math.sqrt(C))
        cross = None
        query_square = None
        for a in range(3):
            wide = spread_heads(query_points[a], mask_q)
            term = mm3(split(wide), split(key_points[a]))
            square = jnp.sum(wide * wide, axis=-1, keepdims=True)
            cross = term if cross is None else cross + term
            query_square = square if query_square is None else query_square + square
        squares = (
            key_points[0] * key_points[0]
            + key_points[1] * key_points[1]
            + key_points[2] * key_points[2]
        )
        selector = jnp.concatenate([mask_q] * owned, axis=0).astype(BF16)
        square_high, square_low = split(squares)
        square_rest = (squares - square_high.astype(F32) - square_low.astype(F32)).astype(BF16)
        key_square = mm(selector, square_high) + (
            mm(selector, square_low) + mm(selector, square_rest)
        )
        distance = query_square + key_square - 2.0 * cross
        biases = bias[...].reshape(owned * HP, count)
        logits = math.sqrt(1.0 / 3.0) * (scores + biases - ps_ref[...] * distance)
        ones = jnp.ones((HP, 1), F32)
        live_row = jnp.concatenate(
            [block[i : i + 1, MASK_AT : MASK_AT + 1] * ones for i in range(owned)], axis=0
        )
        logits = jnp.where(live_row * frame[MASK_AT] > 0.5, logits, MASKED_LOGIT)
        top = jnp.max(logits, axis=-1, keepdims=True)
        weights = jnp.exp(logits - top)
        weights = weights * (1.0 / jnp.sum(weights, axis=-1, keepdims=True))
        weights2 = split(weights)
        rounded = weights2[0]
        scalar_out = pick_heads(mm(rounded, values, NT), mask_c)
        for i in range(owned):
            pair_out[i] = mm(rounded[i * HP : (i + 1) * HP], normed[i])
        moved = [
            pick_heads(mm3(weights2, split(value_points[a]), NT), mask_v) - pos[a]
            for a in range(3)
        ]
        local = [rot[a] * moved[0] + rot[3 + a] * moved[1] + rot[6 + a] * moved[2] for a in range(3)]
        lengths = jnp.sqrt(
            local[0] * local[0] + local[1] * local[1] + local[2] * local[2] + NORM_FLOOR
        )
        pv = H * PV
        mixed = dense(scalar_out, wo2, 0, hc)
        for a in range(3):
            mixed = mixed + dense(local[a], wo2, hc + a * pv, pv)
        mixed = mixed + dense(lengths, wo2, hc + 3 * pv, pv)
        pairs_flat = jnp.concatenate([pair_out[:, h, :] for h in range(H)], axis=-1)
        begin = hc + 4 * pv
        mixed = mixed + dense(pairs_flat, wo2, begin, H * BINS)
        single = layer_norm(own + mixed)
        hidden = jnp.maximum(dense(single, wh2, 0, D), 0.0)
        single = layer_norm(single + dense(hidden, wb2, 0, D))
        update = mm3(split(single), split(wf_ref[...]))
        u = [update[:, k : k + 1] for k in range(6)]
        turn = rotation_from(u[0], u[1], u[2])
        new_rot = [
            rot[3 * a] * turn[b] + rot[3 * a + 1] * turn[3 + b] + rot[3 * a + 2] * turn[6 + b]
            for a in range(3)
            for b in range(3)
        ]
        new_pos = [
            rot[3 * a] * u[3] + rot[3 * a + 1] * u[4] + rot[3 * a + 2] * u[5] + pos[a]
            for a in range(3)
        ]
        place = lax.broadcasted_iota(jnp.int32, (owned, 128), 1)
        packed = block
        for k, entry in enumerate(new_rot + new_pos):
            packed = jnp.where(place == k, entry, packed)
        state[step + 1, :, :D] = single
        state[step + 1, :, D:] = packed

        @pl.when(step < ITERS - 1)
        def _():
            send_state(step + 1)
            gathered[step + 1, my_rows, :D] = single
            gathered[step + 1, my_rows, D:] = packed

        return carry

    lax.fori_loop(0, ITERS, step_body, 0)
    single_ref[...] = state[ITERS, :, :D]
    frames_ref[...] = state[ITERS, :, D:]
    for step in range(ITERS):
        wait_all(step, state_send)
    if ncol > 1:
        part = pairs.at[:, pl.ds(0, (ncol - 1) * col_rows)]
        pltpu.make_async_copy(part, part, pair_send).wait()


def body(
    nrow,
    ncol,
    pair,
    relpos,
    pair_gain,
    bias_weight,
    single,
    rotation_params,
    translation,
    residue_index,
    residue_mask,
    w_scalar,
    w_points,
    head_weights,
    w_out,
    w_hidden,
    w_back,
    w_frame,
):
    owned = single.shape[0]
    count = owned * nrow * ncol
    channels = pair.shape[2]
    out_f = w_out.shape[0]
    rotation = jnp.stack(rotation_from(*rotation_params))
    extra = jnp.concatenate(
        [
            rotation,
            translation,
            residue_index[None].astype(F32),
            residue_mask[None].astype(F32),
            jnp.zeros((WIDE - D - 14, owned), F32),
        ],
        axis=0,
    )
    s0 = jnp.concatenate([single, extra.T], axis=1)
    point_scale = jax.nn.softplus(head_weights) * (math.sqrt(2.0 / (9.0 * PQ)) / 2.0)
    ps = jnp.tile(jnp.pad(point_scale, (0, HP - H)), owned)[:, None]
    bw = jnp.pad(bias_weight.T, ((0, HP - H), (0, 0)))
    vmem = pl.BlockSpec(memory_space=pltpu.VMEM)
    out, frames = pl.pallas_call(
        functools.partial(kernel, nrow, ncol),
        out_shape=(
            jax.ShapeDtypeStruct((owned, D), F32),
            jax.ShapeDtypeStruct((owned, WIDE - D), F32),
        ),
        in_specs=[vmem] * 12,
        out_specs=(vmem, vmem),
        scratch_shapes=[
            pltpu.VMEM((ITERS + 1, owned, WIDE), F32),
            pltpu.VMEM((ITERS, count, WIDE), F32),
            pltpu.VMEM((owned, count, channels), BF16),
            pltpu.VMEM((owned, count, channels), BF16),
            pltpu.VMEM((owned, HP, count), F32),
            pltpu.VMEM((owned, HP, channels), F32),
            pltpu.VMEM((2, w_scalar.shape[1], D), BF16),
            pltpu.VMEM((2, w_points.shape[1], D), BF16),
            pltpu.VMEM((2, out_f, D), BF16),
            pltpu.VMEM((2, D, D), BF16),
            pltpu.VMEM((2, D, D), BF16),
            pltpu.SemaphoreType.DMA,
            pltpu.SemaphoreType.DMA,
            pltpu.SemaphoreType.DMA,
            pltpu.SemaphoreType.DMA((ITERS,)),
            pltpu.SemaphoreType.DMA((ITERS,)),
        ],
        compiler_params=pltpu.CompilerParams(
            collective_id=0, has_side_effects=True, vmem_limit_bytes=58 * 1024 * 1024
        ),
    )(
        s0, pair, relpos, pair_gain[None], bw, ps, w_scalar, w_points, w_out, w_hidden, w_back, w_frame
    )
    return out, frames[:, :12].T


def solution(mesh):
    placed = (
        P("row", "col", None),
        P(),
        P(),
        P(),
        P(("row", "col"), None),
        P(None, ("row", "col")),
        P(None, ("row", "col")),
        P(("row", "col")),
        P(("row", "col")),
        P(),
        P(),
        P(),
        P(),
        P(),
        P(),
        P(),
    )
    return jax.shard_map(
        functools.partial(body, mesh.shape["row"], mesh.shape["col"]),
        mesh=mesh,
        in_specs=placed,
        out_specs=(P(("row", "col"), None), P(None, ("row", "col"))),
        check_vma=False,
    )
```

time: 862 us -> 80.5 us (0.09); the launches traced: 847 us -> 79.9 us
  waiting for transfers between devices: 501 us -> 0 us
  blocking collectives: 139 us -> 0 us
  local copies, waits for them, and re-layouts: 119 us -> 13.1 us
  Pallas kernels: 0 us -> 62.8 us
  matrix products: 43.3 us -> 0 us
  other arithmetic: 29.7 us -> 3.31 us
  between operations: 15.7 us -> 0.66 us
    psum x6 -> x0, waiting for transfers between devices: 501 us -> none  [broadcast(): return lax.psum(jnp.where(mine, value, jnp.zeros_like(value)), axis)]
    all_gather x27 -> x0, blocking collectives: 97.4 us -> none  [the longest x15 58.9 us: joined(): gathered = jax.tree.map(lambda a: lax.all_gather(a, axis), part)]
    unnamed x207 -> x8, local copies, waits for them, and re-layouts: 76.3 us -> 8.82 us
    pallas_call x0 -> x1, Pallas kernels: none -> 62.8 us  [body(): pl.pallas_call(functools.partial(kernel, nrow, ncol), out_shape=(jax.Shap...]
    dot_general x35 -> x0, matrix products: 43.3 us -> none  [the longest x3 7.55 us: advance(): jnp.dot(features.T, w_out, precision=HIGHEST_PRECISION, preferred_element...]
    unnamed x1 -> x0, blocking collectives: 41.6 us -> none
    concatenate x19 -> x1, local copies, waits for them, and re-layouts: 19.9 us -> 0.09 us  [body(): jnp.concatenate([rotation, translation, residue_index[None].astype(F32),...]
    add x22 -> x0, other arithmetic: 9.52 us -> none  [the longest x6 3.39 us: compose(): rotation[3 * left] * update[3] + rotation[3 * left + 1] * update[4]]
  transfers between devices with their start and end apart: 6 -> 0, of which waited for: 6 -> 0; matrix products, arithmetic and copies ran while one was open for 5% -> 0% of each run, Pallas kernels for 0% -> 0%
where the time goes in v1:
time: 80.5 us; the launch traced here: 79.9 us
  Pallas kernels  62.8 us (78%)
  local copies, waits for them, and re-layouts  13.1 us (16%)
  other arithmetic  3.31 us (4%)
    pallas_call x1, Pallas kernels, body(): pl.pallas_call(functools.partial(kernel, nrow, ncol), out_shape=(jax.Shap...  62.8 us
    unnamed x8, local copies, waits for them, and re-layouts  8.82 us

profile of v1, /device:TPU:29, one launch (start us, length us, event | category | flops | bytes accessed | tf_op | source)
XLA Modules:
  0.0 79.9 jit_solution(15634173231849206226)
XLA Ops:
  0.6 0.7 convert_bitcast_fusion.1
  1.3 0.7 convert_bitcast_fusion
  1.9 0.7 fusion
  2.6 0.8 %fusion.1 = (f32[1,8]{1,0:T(1,128)S(1)}, f32[1,8]{1,0:T(1,128)S(1)}, f32[1,8]{1,0:T(1,128)S(1)}) fusion(f32[3,8]{1,0:T(4,128)} %param.21), kind=kLoop, calls=%fused_computation.16 | loop fusion | bytes 192 | tf_op jit(solution)/shard_map/unstack | solution.py:387
  3.4 0.1 copy.28
  3.5 0.1 copy.23
  3.6 0.1 copy.22
  3.7 0.1 copy.29
  3.7 0.1 copy.30
  3.8 1.3 %pad.8.bw_ref = bf16[16,128]{1,0:T(8,128)(2,1)} pad(bf16[12,128]{1,0:T(8,128)(2,1)} %bitcast.10, bf16[]{:T(256)} %constant.12.clone.1), padding=0_4x0_0 | pad | bytes 7170 | tf_op jit(solution)/shard_map/jit(_pad)/pad | solution.py:401
  5.1 0.8 copy.21
  5.9 0.1 concatenate.6
  6.0 1.3 %pad_maximum_fusion.s0_ref = f32[8,512]{1,0:T(8,128)} fusion(f32[8,128]{1,0:T(8,128)S(1)} %bitcast.9, f32[8,384]{1,0:T(8,128)} %param.20), kind=kLoop, calls=%fused_computation | loop fusion | flops 4096 | bytes 32768 | tf_op jit(solution)/shard_map/concatenate | solution.py:398
  7.3 0.7 broadcast_in_dim_tile.4.ps_ref
  8.0 1.5 %copy.27.wf_ref = f32[384,6]{1,0:T(8,128)} copy(f32[384,6]{0,1:T(8,128)} %param.31) | data formatting | bytes 18432 | tf_op args[15]
  9.5 2.5 %copy.25.ws_ref = f32[384,576]{1,0:T(8,128)} copy(f32[384,576]{0,1:T(8,128)} %param.25) | data formatting | bytes 1769472 | tf_op args[9]
  12.0 2.5 %copy.26.wp_ref = f32[384,576]{1,0:T(8,128)} copy(f32[384,576]{0,1:T(8,128)} %param.26) | data formatting | bytes 1769472 | tf_op args[10]
  14.5 62.8 %shard_map.167 = (f32[8,384]{1,0:T(8,128)}, f32[8,128]{1,0:T(8,128)}) custom-call(f32[8,512]{1,0:T(8,128)} %pad_maximum_fusion.s0_ref, bf16[16,128,128]{2,1,0:T(8,128)(2,1)} %pair_ref.1, bf16[128,128]{1,0:T(8,128)(2,1)} %relpos_ref.1, f32[1,128]{1,0:T(1,128)} %bitcast.11, bf16[16,128]{1,0:T(8,128)(2,1)} %pad.8.bw_ref, f32[128,1]{1,0:T(8,128)} %broadcast_in_dim_tile.4.ps_ref, ...), custom_call_target="tpu_custom_call" | custom-call | tf_op jit(solution)/shard_map/pallas_call | solution.py:403
  77.3 1.3 %slice_bitcast_fusion = f32[12,8]{0,1:T(8,128)} fusion(f32[8,128]{1,0:T(8,128)} %get-tuple-element.5), kind=kLoop, calls=%fused_computation.1 | loop fusion | bytes 768 | tf_op jit(solution)/shard_map/transpose | solution.py:435
  78.6 1.3 %copy.32 = f32[8,384]{1,0:T(8,128)} copy(f32[8,384]{1,0:T(8,128)} %get-tuple-element.20) | data formatting | bytes 24576
  (4 shorter events, 0.0 us)

commit v2 on v1

--- a/solution.py
+++ b/solution.py
@@ -27,6 +27,7 @@
 NT = (((1,), (1,)), ((), ()))
 INDEX_AT = 12
 MASK_AT = 13
+PART = 32
 
 
 def rotation_from(quat_b, quat_c, quat_d):
@@ -85,11 +86,15 @@
     nrow,
     ncol,
     s0_ref,
+    params_ref,
+    shift_ref,
+    index_ref,
+    mask_ref,
     pair_ref,
     relpos_ref,
     gain_ref,
     bw_ref,
-    ps_ref,
+    hw_ref,
     ws_ref,
     wp_ref,
     wo_ref,
@@ -98,7 +103,13 @@
     wf_ref,
     single_ref,
     frames_ref,
+    ws_in,
+    wp_in,
+    wo_in,
+    wh_in,
+    wb_in,
     state,
+    outgoing,
     gathered,
     pairs,
     normed,
@@ -114,6 +125,7 @@
     pair_local,
     state_send,
     state_recv,
+    weight_sem,
 ):
     n = nrow * ncol
     row = lax.axis_index("row")
@@ -134,14 +146,13 @@
 
     lax.fori_loop(1, n, greet, 0)
 
-    my_rows = pl.ds(pl.multiple_of(me * owned, owned), owned)
     my_cols = pl.ds(pl.multiple_of(col * col_rows, col_rows), col_rows)
 
     def state_copy(step, k):
         other = lax.rem(me + k, n)
         return pltpu.make_async_remote_copy(
-            src_ref=state.at[step],
-            dst_ref=gathered.at[step, my_rows],
+            src_ref=outgoing.at[step],
+            dst_ref=gathered.at[step, me],
             send_sem=state_send.at[step],
             recv_sem=state_recv.at[step],
             device_id=(other // ncol, lax.rem(other, ncol)),
@@ -156,11 +167,48 @@
         lax.fori_loop(1, n, one, 0)
 
     def wait_all(step, sem):
-        part = gathered.at[step, pl.ds(0, (n - 1) * owned)]
+        part = gathered.at[step, pl.ds(0, n - 1)]
         pltpu.make_async_copy(part, part, sem.at[step]).wait()
 
-    state[0] = s0_ref[...]
-    gathered[0, my_rows] = s0_ref[...]
+    loads = [
+        pltpu.make_async_copy(source, target, weight_sem.at[at])
+        for at, (source, target) in enumerate(
+            ((ws_ref, ws_in), (wp_ref, wp_in), (wo_ref, wo_in), (wh_ref, wh_in), (wb_ref, wb_in))
+        )
+    ]
+    for load in loads:
+        load.start()
+    eye = lax.broadcasted_iota(jnp.int32, (owned, owned), 0) == lax.broadcasted_iota(
+        jnp.int32, (owned, owned), 1
+    )
+
+    def upright(line):
+        return jnp.sum(jnp.where(eye, line, 0.0), axis=1, keepdims=True)
+
+    quat = [upright(params_ref[a : a + 1]) for a in range(3)]
+    start = rotation_from(*quat) + [upright(shift_ref[a : a + 1]) for a in range(3)]
+    start += [upright(index_ref[...].astype(F32)), upright(mask_ref[...].astype(F32))]
+    place = lax.broadcasted_iota(jnp.int32, (owned, WIDE - D), 1)
+    first = jnp.zeros((owned, WIDE - D), F32)
+    for k, entry in enumerate(start):
+        first = jnp.where(place == k, entry, first)
+    own_index = start[INDEX_AT]
+
+    def post(step, values, block):
+        high, low = split(block)
+        rest = (block - high.astype(F32) - low.astype(F32)).astype(BF16)
+        message = (
+            high.astype(F32)
+            + pltpu.roll(low.astype(F32), PART, 1)
+            + pltpu.roll(rest.astype(F32), 2 * PART, 1)
+        )
+        for target in (outgoing.at[step], gathered.at[step, me]):
+            target[:, :D] = values.astype(BF16)
+            target[:, D:] = message.astype(BF16)
+
+    state[0, :, :D] = s0_ref[...]
+    state[0, :, D:] = first
+    post(0, s0_ref[...], first)
     own_pair = pltpu.make_async_copy(
         pair_ref.at[pl.ds(col * owned, owned)], pairs.at[:, my_cols], pair_local
     )
@@ -178,17 +226,23 @@
             device_id_type=MESH,
         ).start()
 
-    for source, target in ((ws_ref, wst), (wp_ref, wpt)):
-        total = source.shape[1]
-        for begin in range(0, total, 128):
-            end = min(begin + 128, total)
-            high, low = split(source[:, begin:end].T)
-            target[0, begin:end] = high
-            target[1, begin:end] = low
-    for source, target in ((wo_ref, wo2), (wh_ref, wh2), (wb_ref, wb2)):
+    for load, source, target in zip(
+        loads, (ws_in, wp_in, wo_in, wh_in, wb_in), (wst, wpt, wo2, wh2, wb2)
+    ):
+        load.wait()
         high, low = split(source[...])
         target[0] = high
         target[1] = low
+    heads = hw_ref[...]
+    heads = jnp.maximum(heads, 0.0) + jnp.log1p(jnp.exp(-jnp.abs(heads)))
+    heads = heads * (math.sqrt(2.0 / (9.0 * PQ)) / 2.0)
+    here = lax.broadcasted_iota(jnp.int32, (HP, H), 0) == lax.broadcasted_iota(
+        jnp.int32, (HP, H), 1
+    )
+    point_scale = jnp.concatenate(
+        [jnp.sum(jnp.where(here, heads, 0.0), axis=1, keepdims=True)] * owned, axis=0
+    )
+    bias[...] = jnp.zeros_like(bias)
 
     own_pair.wait()
     if ncol > 1:
@@ -196,9 +250,11 @@
         pltpu.make_async_copy(part, part, pair_recv).wait()
     wait_all(0, state_recv)
 
-    index_col = gathered[0, :, D : D + 128][:, INDEX_AT : INDEX_AT + 1]
+    blocks = gathered[0, :, :, D:].astype(F32).reshape(count, WIDE - D)
+    index_col = sum(
+        blocks[:, at : at + 1] for at in range(INDEX_AT, INDEX_AT + 3 * PART, PART)
+    )
     lanes = lax.broadcasted_iota(jnp.int32, (count, BINS), 1).astype(F32)
-    own_index = s0_ref[:, D:][:, INDEX_AT : INDEX_AT + 1]
     sublanes = lax.broadcasted_iota(jnp.int32, (owned, 1), 0)
     relpos = relpos_ref[...]
     gain = gain_ref[...]
@@ -211,7 +267,7 @@
         summed = pairs[i].astype(F32) + mm(onehot, relpos)
         rows = (layer_norm(summed) * gain).astype(BF16)
         normed[i] = rows
-        bias[i] = mm(bw, rows, NT)
+        bias[i, :H] = mm(bw, rows, NT)
         return carry
 
     lax.fori_loop(0, owned, prepare, 0)
@@ -227,9 +283,12 @@
         def _():
             wait_all(step, state_recv)
 
-        turned = gathered[step].T
-        x = split(turned[:D])
-        frame = [turned[D + k : D + k + 1] for k in range(14)]
+        turned = gathered[step].astype(F32).reshape(count, WIDE).T
+        x = turned[:D].astype(BF16)
+        joined = turned[D : D + 16] + (
+            turned[D + PART : D + PART + 16] + turned[D + 2 * PART : D + 2 * PART + 16]
+        )
+        frame = [joined[k : k + 1] for k in range(14)]
         mine = state[step]
         own = mine[:, :D]
         block = mine[:, D:]
@@ -237,10 +296,10 @@
         pos = [block[:, 9 + k : 10 + k] for k in range(3)]
         own2 = split(own)
         hc = H * C
-        keyval = mm3((wst[0, hc:], wst[1, hc:]), x).astype(BF16)
+        keyval = (mm(wst[0, hc:], x) + mm(wst[1, hc:], x)).astype(BF16)
         keys, values = keyval[:hc], keyval[hc:]
         kp = 3 * H * PQ
-        locals_t = mm3((wpt[0, kp:], wpt[1, kp:]), x)
+        locals_t = mm(wpt[0, kp:], x) + mm(wpt[1, kp:], x)
 
         def lift(base, width):
             p = [locals_t[base + a * width : base + (a + 1) * width] for a in range(3)]
@@ -290,7 +349,7 @@
         )
         distance = query_square + key_square - 2.0 * cross
         biases = bias[...].reshape(owned * HP, count)
-        logits = math.sqrt(1.0 / 3.0) * (scores + biases - ps_ref[...] * distance)
+        logits = math.sqrt(1.0 / 3.0) * (scores + biases - point_scale * distance)
         ones = jnp.ones((HP, 1), F32)
         live_row = jnp.concatenate(
             [block[i : i + 1, MASK_AT : MASK_AT + 1] * ones for i in range(owned)], axis=0
@@ -323,7 +382,7 @@
         single = layer_norm(own + mixed)
         hidden = jnp.maximum(dense(single, wh2, 0, D), 0.0)
         single = layer_norm(single + dense(hidden, wb2, 0, D))
-        update = mm3(split(single), split(wf_ref[...]))
+        update = mm3(split(single), split(wf_ref[...]), NT)
         u = [update[:, k : k + 1] for k in range(6)]
         turn = rotation_from(u[0], u[1], u[2])
         new_rot = [
@@ -335,7 +394,6 @@
             rot[3 * a] * u[3] + rot[3 * a + 1] * u[4] + rot[3 * a + 2] * u[5] + pos[a]
             for a in range(3)
         ]
-        place = lax.broadcasted_iota(jnp.int32, (owned, 128), 1)
         packed = block
         for k, entry in enumerate(new_rot + new_pos):
             packed = jnp.where(place == k, entry, packed)
@@ -344,15 +402,14 @@
 
         @pl.when(step < ITERS - 1)
         def _():
+            post(step + 1, single, packed)
             send_state(step + 1)
-            gathered[step + 1, my_rows, :D] = single
-            gathered[step + 1, my_rows, D:] = packed
 
         return carry
 
     lax.fori_loop(0, ITERS, step_body, 0)
     single_ref[...] = state[ITERS, :, :D]
-    frames_ref[...] = state[ITERS, :, D:]
+    frames_ref[...] = state[ITERS, :, D:][:, :12]
     for step in range(ITERS):
         wait_all(step, state_send)
     if ncol > 1:
@@ -384,33 +441,25 @@
     count = owned * nrow * ncol
     channels = pair.shape[2]
     out_f = w_out.shape[0]
-    rotation = jnp.stack(rotation_from(*rotation_params))
-    extra = jnp.concatenate(
-        [
-            rotation,
-            translation,
-            residue_index[None].astype(F32),
-            residue_mask[None].astype(F32),
-            jnp.zeros((WIDE - D - 14, owned), F32),
-        ],
-        axis=0,
-    )
-    s0 = jnp.concatenate([single, extra.T], axis=1)
-    point_scale = jax.nn.softplus(head_weights) * (math.sqrt(2.0 / (9.0 * PQ)) / 2.0)
-    ps = jnp.tile(jnp.pad(point_scale, (0, HP - H)), owned)[:, None]
-    bw = jnp.pad(bias_weight.T, ((0, HP - H), (0, 0)))
     vmem = pl.BlockSpec(memory_space=pltpu.VMEM)
+    away = pl.BlockSpec(memory_space=pl.ANY)
     out, frames = pl.pallas_call(
         functools.partial(kernel, nrow, ncol),
         out_shape=(
             jax.ShapeDtypeStruct((owned, D), F32),
-            jax.ShapeDtypeStruct((owned, WIDE - D), F32),
+            jax.ShapeDtypeStruct((owned, 12), F32),
         ),
-        in_specs=[vmem] * 12,
+        in_specs=[vmem] * 10 + [away] * 5 + [vmem],
         out_specs=(vmem, vmem),
         scratch_shapes=[
+            pltpu.VMEM((w_scalar.shape[1], D), F32),
+            pltpu.VMEM((w_points.shape[1], D), F32),
+            pltpu.VMEM((out_f, D), F32),
+            pltpu.VMEM((D, D), F32),
+            pltpu.VMEM((D, D), F32),
             pltpu.VMEM((ITERS + 1, owned, WIDE), F32),
-            pltpu.VMEM((ITERS, count, WIDE), F32),
+            pltpu.VMEM((ITERS, owned, WIDE), BF16),
+            pltpu.VMEM((ITERS, count // owned, owned, WIDE), BF16),
             pltpu.VMEM((owned, count, channels), BF16),
             pltpu.VMEM((owned, count, channels), BF16),
             pltpu.VMEM((owned, HP, count), F32),
@@ -425,14 +474,30 @@
             pltpu.SemaphoreType.DMA,
             pltpu.SemaphoreType.DMA((ITERS,)),
             pltpu.SemaphoreType.DMA((ITERS,)),
+            pltpu.SemaphoreType.DMA((5,)),
         ],
         compiler_params=pltpu.CompilerParams(
             collective_id=0, has_side_effects=True, vmem_limit_bytes=58 * 1024 * 1024
         ),
     )(
-        s0, pair, relpos, pair_gain[None], bw, ps, w_scalar, w_points, w_out, w_hidden, w_back, w_frame
-    )
-    return out, frames[:, :12].T
+        single,
+        rotation_params,
+        translation,
+        residue_index[None],
+        residue_mask[None],
+        pair,
+        relpos,
+        pair_gain[None],
+        bias_weight.T,
+        head_weights[None],
+        w_scalar.T,
+        w_points.T,
+        w_out,
+        w_hidden,
+        w_back,
+        w_frame.T,
+    )
+    return out, frames.T
 
 
 def solution(mesh):

time: 80.5 us -> 50.7 us (0.63)
  Pallas kernels: 62.8 us -> 46.7 us
  local copies, waits for them, and re-layouts: 13.1 us -> 2.57 us
  other arithmetic: 3.31 us -> 0 us
    pallas_call x1, Pallas kernels: 62.8 us -> 46.7 us  [body(): pl.pallas_call(functools.partial(kernel, nrow, ncol), out_shape=(jax.Shap...]
    unnamed x8 -> x2, local copies, waits for them, and re-layouts: 8.82 us -> 2.57 us
    another operation x3 -> x0, local copies, waits for them, and re-layouts: 1.51 us -> none  [the longest x1 0.8 us: body(): rotation = jnp.stack(rotation_from(*rotation_params))]
    concatenate x1 -> x0, other arithmetic: 1.32 us -> none  [body(): s0 = jnp.concatenate([single, extra.T], axis=1)]
    convert_element_type x2 -> x0, other arithmetic: 1.32 us -> none  [the longest x1 0.66 us: body(): residue_index[None].astype(F32)]
    pad x2 -> x0, local copies, waits for them, and re-layouts: 1.29 us -> none  [the longest x1 1.28 us: body(): bw = jnp.pad(bias_weight.T, ((0, HP - H), (0, 0)))]
    transpose x1 -> x0, local copies, waits for them, and re-layouts: 1.27 us -> none  [body(): return (out, frames[:, :12].T)]
where the time goes in v2:
time: 50.7 us; the launch traced here: 49.9 us
  Pallas kernels  46.7 us (92%)
  local copies, waits for them, and re-layouts  2.57 us (5%)
  between operations  0.65 us (1%)
    pallas_call x1, Pallas kernels, body(): pl.pallas_call(functools.partial(kernel, nrow, ncol), out_shape=(jax.Shap...  46.7 us
    unnamed x2, local copies, waits for them, and re-layouts  2.57 us

profile of v2, /device:TPU:29, one launch (start us, length us, event | category | flops | bytes accessed | tf_op | source)
XLA Modules:
  0.0 49.9 jit_solution(16527974704950091743)
XLA Ops:
  0.6 46.7 %shard_map.167 = (f32[8,384]{1,0:T(8,128)}, f32[8,12]{1,0:T(8,128)}) custom-call(f32[8,384]{1,0:T(8,128)} %s0_ref.1, f32[3,8]{1,0:T(4,128)} %params_ref.1, f32[3,8]{1,0:T(4,128)} %shift_ref.1, s32[1,8]{1,0:T(1,128)} %bitcast.14, s32[1,8]{1,0:T(1,128)} %bitcast.15, bf16[16,128,128]{2,1,0:T(8,128)(2,1)} %pair_ref.1, bf16[128,128]{1,0:T(8,128)(2,1)} %relpos_ref.1, ...), custom_call_target="tpu_custom_call" | custom-call | tf_op jit(solution)/shard_map/pallas_call | solution.py:446
  47.4 1.3 %copy.20 = f32[8,384]{1,0:T(8,128)} copy(f32[8,384]{1,0:T(8,128)} %get-tuple-element.8) | data formatting | bytes 24576
  48.7 1.3 %copy.21 = f32[12,8]{0,1:T(8,128)} copy(f32[12,8]{0,1:T(8,128)} %bitcast.13) | data formatting | bytes 768
